TPU v7x, 32 devices: a whole 2x2x4 slice. The times are simulated.
32 devices in a mesh: row: 4 (over x, core), col: 8 (over z, y).
Axes of the slice: x: 2, y: 2, z: 4, core: 2. Of those that a mesh axis runs over, the one named last changes fastest.
Arguments:
- inputs: bfloat16 [512, 8192], P('col', 'row'), may hold values from -6 to 6
- cotangent: bfloat16 [512, 8192], P('col', 'row'), may hold values from -6 to 6
- gate_pre: bfloat16 [512, 16384], P('row', 'col'), may hold values from -8 to 8
- up_pre: bfloat16 [512, 16384], P('row', 'col'), may hold values from -6 to 6
- w_gate: bfloat16 [8192, 16384], P('row', 'col'), may hold values from -0.0625 to 0.0625
- w_up: bfloat16 [8192, 16384], P('row', 'col'), may hold values from -0.0625 to 0.0625
- w_down: bfloat16 [16384, 8192], P('col', 'row'), may hold values from -0.046875 to 0.046875
Outputs:
- grad_inputs: bfloat16 [512, 8192], P('col', 'row')
- grad_gate: float32 [8192, 16384], P('row', 'col')
- grad_up: float32 [8192, 16384], P('row', 'col')
- grad_down: float32 [16384, 8192], P('col', 'row')
All inputs are finite; a program needn't handle non-finite values.
Results may differ from a plain program's by a relative error of at most 0.0049.
Values may be sent and summed in bfloat16 or wider, within the bound.
A program may use at most 128 MiB of HBM per device.

v0:
```python
import math

import jax
import jax.numpy as jnp
from jax import lax
from jax.sharding import PartitionSpec as P


def swiglu_back(gate_pre, up_pre, grad_hidden):
    gate_f = gate_pre.astype(jnp.float32)
    up_f = up_pre.astype(jnp.float32)
    sig = jax.nn.sigmoid(gate_f)
    act = gate_f * sig
    hidden = (act * up_f).astype(jnp.bfloat16)
    grad_gate_pre = (grad_hidden * up_f * sig * (1.0 + gate_f * (1.0 - sig))).astype(jnp.bfloat16)
    grad_up_pre = (grad_hidden * act).astype(jnp.bfloat16)
    return (hidden, grad_gate_pre, grad_up_pre)


def contract_last(left, right):
    return lax.dot_general(
        left, right, (((1,), (1,)), ((), ())), preferred_element_type=jnp.float32
    )


def contract_first(left, right):
    return lax.dot_general(
        left, right, (((0,), (0,)), ((), ())), preferred_element_type=jnp.float32
    )


def per_device(inputs, cotangent, gate_pre, up_pre, w_gate, w_up, w_down):
    inputs_all, cotan_all = (
        lax.all_gather(inputs, "col", axis=0, tiled=True),
        lax.all_gather(cotangent, "col", axis=0, tiled=True),
    )
    grad_hidden = lax.psum_scatter(
        contract_last(cotan_all, w_down), "row", scatter_dimension=0, tiled=True
    )
    hidden, grad_gate_pre, grad_up_pre = swiglu_back(gate_pre, up_pre, grad_hidden)
    hidden_all, gate_grad_all, up_grad_all = (
        lax.all_gather(hidden, "row", axis=0, tiled=True),
        lax.all_gather(grad_gate_pre, "row", axis=0, tiled=True),
        lax.all_gather(grad_up_pre, "row", axis=0, tiled=True),
    )
    grad_inputs = lax.psum_scatter(
        contract_last(gate_grad_all, w_gate) + contract_last(up_grad_all, w_up),
        "col",
        scatter_dimension=0,
        tiled=True,
    )
    scale = 1.0 / math.sqrt(inputs_all.shape[0])
    grad_gate = contract_first(inputs_all, gate_grad_all) * scale
    grad_up = contract_first(inputs_all, up_grad_all) * scale
    grad_down = contract_first(hidden_all, cotan_all) * scale
    return (grad_inputs.astype(jnp.bfloat16), grad_gate, grad_up, grad_down)


def solution(mesh):
    in_specs = (
        P("col", "row"),
        P("col", "row"),
        P("row", "col"),
        P("row", "col"),
        P("row", "col"),
        P("row", "col"),
        P("col", "row"),
    )
    out_specs = (P("col", "row"), P("row", "col"), P("row", "col"), P("col", "row"))
    return jax.shard_map(
        per_device, mesh=mesh, in_specs=in_specs, out_specs=out_specs, check_vma=False
    )
```

profile of v0, /device:TPU:0, one launch (start us, length us, event | category | flops | bytes accessed | tf_op | source)
XLA Modules:
  0.0 340.3 jit_solution(5187956274251306020)
XLA Ops:
  7.2 0.7 all-gather.6.cloned.1.call-update
  7.9 0.0 reduce-scatter.3.cloned.1.call-start
  7.9 54.0 %all-gather.6.cloned.1.call-done = bf16[512,2048]{1,0:T(8,128)(2,1)} async-done(((bf16[64,2048]{1,0:T(8,128)(2,1)}), bf16[512,2048]{1,0:T(8,128)(2,1)}) %all-gather.6.cloned.1.call-update) | async-done | bytes 2097168 | tf_op jit(solution)/shard_map/all_gather | solution.py:35
  61.9 10.6 %fusion.8 = f32[512,2048]{1,0:T(8,128)} fusion(bf16[512,2048]{1,0:T(8,128)(2,1)} %all-gather.6.cloned.1.call-done, bf16[2048,2048]{1,0:T(8,128)(2,1)} %param.13), kind=kOutput, calls=%fused_computation.18 | convolution fusion | flops 4294967296 | bytes 14680064 | tf_op jit(solution)/shard_map/dot_general | solution.py:21
  72.5 0.0 all-gather.8.cloned.1.call-start
  72.6 43.2 %reduce-scatter.3.cloned.1.call-done = f32[128,2048]{1,0:T(8,128)} async-done(((f32[512,2048]{1,0:T(8,128)}), f32[128,2048]{1,0:T(8,128)}) %reduce-scatter.3.cloned.1.call-update) | async-done | bytes 1048592 | tf_op jit(solution)/shard_map/reduce_scatter | solution.py:37
  115.8 2.9 multiply_convert_fusion
  118.8 0.0 all-gather.10.cloned.1.call-start
  118.8 0.5 all-gather.10.cloned.1.call-update
  119.4 0.5 all-gather.12.cloned.1.call-update
  120.0 0.5 all-gather.14.cloned.1.call-update
  120.5 0.2 reduce-scatter.5.cloned.1.call-start
  120.7 20.7 %all-gather.8.cloned.1.call-done = bf16[512,2048]{1,0:T(8,128)(2,1)} async-done(((bf16[128,2048]{1,0:T(8,128)(2,1)}), bf16[512,2048]{1,0:T(8,128)(2,1)}) %all-gather.8.cloned.1.call-update) | async-done | bytes 2097168 | tf_op jit(solution)/shard_map/all_gather | solution.py:43
  141.5 10.6 %fusion.9 = f32[512,2048]{1,0:T(8,128)} fusion(bf16[512,2048]{1,0:T(8,128)(2,1)} %all-gather.8.cloned.1.call-done, bf16[2048,2048]{1,0:T(8,128)(2,1)} %param.11), kind=kOutput, calls=%fused_computation.19 | convolution fusion | flops 4294967296 | bytes 14680064 | tf_op jit(solution)/shard_map/dot_general | solution.py:21
  152.0 14.0 %all-gather.10.cloned.1.call-done = bf16[512,2048]{1,0:T(8,128)(2,1)} async-done(((bf16[128,2048]{1,0:T(8,128)(2,1)}), bf16[512,2048]{1,0:T(8,128)(2,1)}) %all-gather.10.cloned.1.call-update) | async-done | bytes 2097168 | tf_op jit(solution)/shard_map/all_gather | solution.py:44
  166.1 11.6 %convolution_add_fusion = f32[512,2048]{1,0:T(8,128)} fusion(f32[512,2048]{1,0:T(8,128)} %fusion.9, bf16[512,2048]{1,0:T(8,128)(2,1)} %all-gather.10.cloned.1.call-done, bf16[2048,2048]{1,0:T(8,128)(2,1)} %param.12), kind=kOutput, calls=%fused_computation.3 | convolution fusion | flops 4296015872 | bytes 18874368 | tf_op jit(solution)/shard_map/dot_general | solution.py:21
  177.7 39.4 %all-gather.12.cloned.1.call-done = bf16[512,2048]{1,0:T(8,128)(2,1)} async-done(((bf16[64,2048]{1,0:T(8,128)(2,1)}), bf16[512,2048]{1,0:T(8,128)(2,1)}) %all-gather.12.cloned.1.call-update) | async-done | bytes 2097168 | tf_op jit(solution)/shard_map/all_gather | solution.py:34
  217.2 10.1 %multiply_bitcast_fusion.1 = f32[2048,2048]{0,1:T(8,128)} fusion(bf16[512,2048]{1,0:T(8,128)(2,1)S(1)} %copy-done.3, bf16[512,2048]{1,0:T(8,128)(2,1)} %all-gather.12.cloned.1.call-done), kind=kOutput, calls=%fused_computation.1 | convolution fusion | flops 4299161600 | bytes 20971520 | tf_op jit(solution)/shard_map/dot_general | solution.py:27
  227.3 17.8 %copy.11 = f32[2048,2048]{1,0:T(8,128)} copy(f32[2048,2048]{0,1:T(8,128)} %multiply_bitcast_fusion.1) | data formatting | bytes 33554432
  245.1 10.1 %multiply_bitcast_fusion = f32[2048,2048]{0,1:T(8,128)} fusion(bf16[512,2048]{1,0:T(8,128)(2,1)S(1)} %copy-done.4, bf16[512,2048]{1,0:T(8,128)(2,1)} %all-gather.12.cloned.1.call-done), kind=kOutput, calls=%fused_computation | convolution fusion | flops 4299161600 | bytes 20971520 | tf_op jit(solution)/shard_map/dot_general | solution.py:27
  255.2 17.9 %copy.12 = f32[2048,2048]{1,0:T(8,128)} copy(f32[2048,2048]{0,1:T(8,128)} %multiply_bitcast_fusion) | data formatting | bytes 33554432
  273.1 10.2 %convolution_multiply_fusion = f32[2048,2048]{1,0:T(8,128)} fusion(bf16[512,2048]{1,0:T(8,128)(2,1)} %all-gather.14.cloned.1.call-done, bf16[512,2048]{1,0:T(8,128)(2,1)S(1)} %copy-done.2), kind=kOutput, calls=%fused_computation.2 | convolution fusion | flops 4299161600 | bytes 20971520 | tf_op jit(solution)/shard_map/dot_general | solution.py:27
  283.2 48.4 %reduce-scatter.5.cloned.1.call-done = f32[64,2048]{1,0:T(8,128)} async-done(((f32[512,2048]{1,0:T(8,128)}), f32[64,2048]{1,0:T(8,128)}) %reduce-scatter.5.cloned.1.call-update) | async-done | bytes 524304 | tf_op jit(solution)/shard_map/reduce_scatter | solution.py:46
  331.7 1.8 convert_element_type.22
  (17 shorter events, 0.2 us)
Async XLA Ops:
  7.2 54.8 %all-gather.6.cloned.1.call-start = ((), (), s32[]{:S(2)}) async-start(), calls=%async_computation.2 | async-start | bytes 2359296 | tf_op jit(solution)/shard_map/all_gather | solution.py:35
  7.9 107.9 %reduce-scatter.3.cloned.1.call-start = ((), (), s32[]{:S(2)}) async-start(), calls=%async_computation.3 | async-start | bytes 5242880 | tf_op jit(solution)/shard_map/reduce_scatter | solution.py:37
  72.5 43.3 %copy-start = (bf16[128,2048]{1,0:T(8,128)(2,1)S(1)}, bf16[128,2048]{1,0:T(8,128)(2,1)}, u32[]{:S(2)}) copy-start(bf16[128,2048]{1,0:T(8,128)(2,1)} %param.9) | copy-start | bytes 1572868
  72.5 43.3 %copy-start.1 = (bf16[128,2048]{1,0:T(8,128)(2,1)S(1)}, bf16[128,2048]{1,0:T(8,128)(2,1)}, u32[]{:S(2)}) copy-start(bf16[128,2048]{1,0:T(8,128)(2,1)} %param.10) | copy-start | bytes 1572868
  72.5 68.9 %all-gather.8.cloned.1.call-start = ((), (), s32[]{:S(2)}) async-start(), calls=%async_computation.4 | async-start | bytes 2621440 | tf_op jit(solution)/shard_map/all_gather | solution.py:43
  118.8 47.3 %all-gather.10.cloned.1.call-start = ((), (), s32[]{:S(2)}) async-start(), calls=%async_computation.5 | async-start | bytes 2621440 | tf_op jit(solution)/shard_map/all_gather | solution.py:44
  119.3 97.8 %all-gather.12.cloned.1.call-start = ((), (), s32[]{:S(2)}) async-start(), calls=%async_computation.7 | async-start | bytes 2359296 | tf_op jit(solution)/shard_map/all_gather | solution.py:34
  119.9 153.2 %all-gather.14.cloned.1.call-start = ((), (), s32[]{:S(2)}) async-start(), calls=%async_computation.8 | async-start | bytes 2621440 | tf_op jit(solution)/shard_map/all_gather | solution.py:42
  120.5 211.2 %reduce-scatter.5.cloned.1.call-start = ((), (), s32[]{:S(2)}) async-start(), calls=%async_computation.6 | async-start | bytes 4718592 | tf_op jit(solution)/shard_map/reduce_scatter | solution.py:46
  177.7 39.5 %copy-start.3 = (bf16[512,2048]{1,0:T(8,128)(2,1)S(1)}, bf16[512,2048]{1,0:T(8,128)(2,1)}, u32[]{:S(2)}) copy-start(bf16[512,2048]{1,0:T(8,128)(2,1)} %all-gather.8.cloned.1.call-done) | copy-start | bytes 6291460
  227.3 17.8 %copy-start.4 = (bf16[512,2048]{1,0:T(8,128)(2,1)S(1)}, bf16[512,2048]{1,0:T(8,128)(2,1)}, u32[]{:S(2)}) copy-start(bf16[512,2048]{1,0:T(8,128)(2,1)} %all-gather.10.cloned.1.call-done) | copy-start | bytes 6291460
  255.2 17.9 %copy-start.2 = (bf16[512,2048]{1,0:T(8,128)(2,1)S(1)}, bf16[512,2048]{1,0:T(8,128)(2,1)}, u32[]{:S(2)}) copy-start(bf16[512,2048]{1,0:T(8,128)(2,1)} %all-gather.6.cloned.1.call-done) | copy-start | bytes 6291460
Sparse Core Ops, SparseCore 0:
  10.1 51.7 all-gather.5
  72.7 43.1 reduce-scatter.2
  118.9 22.5 all-gather.7
  143.5 22.5 all-gather.9
  168.0 49.0 all-gather.11
  218.6 21.0 all-gather.13
  243.3 88.2 reduce-scatter.4
where the time goes:
time: 341 us; the launch traced here: 340 us
  waiting for transfers between devices  222 us (65%)
  matrix products  63.2 us (19%)
  local copies, waits for them, and re-layouts  35.6 us (10%)
  between operations  14.1 us (4%)
  other arithmetic  4.69 us (1%)
    all_gather x1, waiting for transfers between devices, per_device(): lax.all_gather(cotangent, 'col', axis=0, tiled=True)  54 us
    reduce_scatter x1, waiting for transfers between devices, per_device(): lax.psum_scatter(contract_last(gate_grad_all, w_gate) + contract_last(up_...  48.4 us
    reduce_scatter x1, waiting for transfers between devices, per_device(): lax.psum_scatter(contract_last(cotan_all, w_down), 'row', scatter_dimensi...  43.2 us
    all_gather x1, waiting for transfers between devices, per_device(): lax.all_gather(inputs, 'col', axis=0, tiled=True)  39.4 us
    unnamed x12, local copies, waits for them, and re-layouts  35.6 us
    dot_general x3, matrix products, contract_last(): lax.dot_general(left, right, (((1,), (1,)), ((), ())), preferred_element_...  32.8 us
    dot_general x3, matrix products, contract_first(): lax.dot_general(left, right, (((0,), (0,)), ((), ())), preferred_element_...  30.4 us
    all_gather x1, waiting for transfers between devices, per_device(): lax.all_gather(grad_gate_pre, 'row', axis=0, tiled=True)  20.7 us
  transfers between devices with their start and end apart: 7, of which 6 were waited for; matrix products, arithmetic and copies ran while one was open for 26% of the time, Pallas kernels for 0%

commit v1 on v0

v1 whole, which is shorter than its diff:
```python
import math

import jax
import jax.numpy as jnp
from jax import lax
from jax.experimental import pallas as pl
from jax.experimental.pallas import tpu as pltpu
from jax.sharding import PartitionSpec as P


F32 = jnp.float32
BF16 = jnp.bfloat16
GRANT = 60 * 1024 * 1024


def tile_of(extent, most):
    tile = min(extent, most)
    while extent % tile:
        tile //= 2
    return tile


def resident(shape):
    return pl.BlockSpec(shape, lambda i: (0,) * len(shape))


def call(body, operands, in_specs, outs, out_specs, scratch, steps, flops):
    moved = sum(a.size * a.dtype.itemsize for a in list(operands) + list(outs))
    return pl.pallas_call(
        body,
        grid=(steps,),
        in_specs=in_specs,
        out_specs=out_specs,
        scratch_shapes=scratch,
        out_shape=outs,
        compiler_params=pltpu.CompilerParams(
            dimension_semantics=("arbitrary",), vmem_limit_bytes=GRANT
        ),
        cost_estimate=pl.CostEstimate(flops=flops, bytes_accessed=moved, transcendentals=0),
    )(*operands)


def dot_nt(left, right):
    return lax.dot_general(left, right, (((1,), (1,)), ((), ())), preferred_element_type=F32)


def where(rows, cols):
    groups, lines = rows // 2, cols // 2
    r, c = lax.axis_index("row"), lax.axis_index("col")
    g, core, z, y = lax.div(r, 2), lax.rem(r, 2), lax.div(c, 2), lax.rem(c, 2)
    back = [lax.rem(z - k + lines, lines) for k in range(lines)]
    ahead = [lax.rem(z + k, lines) for k in range(lines)]
    ring = [lax.rem(g + j, groups) for j in range(groups)]
    col_at = [2 * v + y for v in back] + [2 * v + 1 - y for v in back]
    row_at = [2 * v + core for v in ring] + [2 * v + 1 - core for v in ring]
    pick = [2 * v + 1 - y for v in ahead] + [2 * v + y for v in ahead]
    return col_at, row_at, pick


def hidden_grad(mesh, blocks, w_down, part, parts):
    rows, cols = mesh
    count, depth, wide = len(blocks), blocks[0].shape[-1], w_down.shape[0] // parts
    chunk, fresh = blocks[0].shape[0], count > 1
    tokens, tile = count * chunk, tile_of(wide, 256)
    per, half, steps = tokens // rows, rows // 2, wide // tile

    def body(*refs):
        ins, w, mine, theirs, total = refs[:count], refs[count], *refs[count + 1:count + 3], refs[-1]
        col_at, row_at, _ = where(rows, cols)
        if fresh:
            held = refs[count + 3]

            @pl.when(pl.program_id(0) == 0)
            def _():
                for at, ref in zip(col_at, ins):
                    held[at] = ref[...]

            left = held[...].reshape(tokens, depth)
        else:
            left = ins[0][...]
        total[...] = dot_nt(left, w[...]).reshape(rows, per, tile)
        for j in range(half):
            mine[j] = total[row_at[j]]
            theirs[j] = total[row_at[half + j]]

    outs = [jax.ShapeDtypeStruct((half, per, wide), F32)] * 2
    out_specs = [pl.BlockSpec((half, per, tile), lambda i: (0, 0, i))] * 2
    if fresh:
        outs.append(jax.ShapeDtypeStruct((count, chunk, depth), BF16))
        out_specs.append(resident((count, chunk, depth)))
    got = call(
        body, (*blocks, w_down),
        [resident((chunk, depth))] * count
        + [pl.BlockSpec((tile, depth), lambda i: (i + part * steps, 0))],
        outs, out_specs, [pltpu.VMEM((rows, per, tile), F32)], steps, 2 * tokens * depth * wide,
    )
    return got[0], got[1], (got[2].reshape(tokens, depth) if fresh else blocks[0])


def input_grad(mesh, gates, ups, w_gate, w_up, part, parts):
    rows, cols = mesh
    fresh = len(gates) > 1
    count, depth, wide = len(gates), w_gate.shape[1], w_gate.shape[0] // parts
    tokens = rows * gates[0].shape[1] if fresh else gates[0].shape[0]
    tile, half, lines = tile_of(wide, 256), rows // 2, cols // 2
    per, steps, block = tokens // cols, wide // tile, tokens // rows

    def body(*refs):
        wg, wu, send, keep = refs[2 * count:2 * count + 4]
        _, row_at, pick = where(rows, cols)
        if fresh:
            wholes = refs[2 * count + 4:2 * count + 6]

            @pl.when(pl.program_id(0) == 0)
            def _():
                for whole, ins in zip(wholes, (refs[:count], refs[count:2 * count])):
                    for n, ref in enumerate(ins):
                        width = ref.shape[-1]
                        at = n // 2 * width
                        for j in range(half):
                            whole[row_at[n % 2 * half + j], :, at:at + width] = ref[j]

            left = [w[...].reshape(tokens, depth) for w in wholes]
        else:
            left = [refs[0][...], refs[1][...]]
        total = refs[-1]
        total[...] = (dot_nt(left[0], wg[...]) + dot_nt(left[1], wu[...])).reshape(cols, per, tile)
        for k in range(lines):
            send[k] = total[pick[k]].astype(BF16)
            keep[k] = total[pick[lines + k]]

    weight = pl.BlockSpec((tile, depth), lambda i: (i + part * steps, 0))
    outs = [jax.ShapeDtypeStruct((lines, per, wide), t) for t in (BF16, F32)]
    out_specs = [pl.BlockSpec((lines, per, tile), lambda i: (0, 0, i))] * 2
    if fresh:
        outs += [jax.ShapeDtypeStruct((rows, block, depth), BF16)] * 2
        out_specs += [resident((rows, block, depth))] * 2
    got = call(
        body, (*gates, *ups, w_gate, w_up),
        [resident(a.shape) for a in (*gates, *ups)] + [weight] * 2,
        outs, out_specs, [pltpu.VMEM((cols, per, tile), F32)], steps, 4 * tokens * depth * wide,
    )
    if not fresh:
        return got[0], got[1], gates[0], ups[0]
    return got[0], got[1], got[2].reshape(tokens, depth), got[3].reshape(tokens, depth)


def outer(mesh, left, by_row, right, scale):
    rows, cols = mesh
    tokens, wide = right.shape
    count, spread = len(left), left[0].shape[-1]
    tile, size = tile_of(spread, 256), left[0].shape[1]
    every = sum(a.shape[0] for a in left)

    def body(*refs):
        right_ref, out, held = refs[count:]
        at = where(rows, cols)[1 if by_row else 0]
        n = 0
        for ref in refs[:count]:
            for j in range(ref.shape[0]):
                held[at[n]] = ref[j]
                n += 1
        out[...] = lax.dot_general(
            held[...].reshape(tokens, tile), right_ref[...],
            (((0,), (0,)), ((), ())), preferred_element_type=F32,
        ) * scale

    return call(
        body, (*left, right),
        [pl.BlockSpec((a.shape[0], size, tile), lambda i: (0, 0, i)) for a in left]
        + [resident((tokens, wide))],
        [jax.ShapeDtypeStruct((spread, wide), F32)],
        [pl.BlockSpec((tile, wide), lambda i: (i, 0))],
        [pltpu.VMEM((every, size, tile), BF16)], spread // tile, 2 * tokens * spread * wide,
    )[0]


PARTS = 2


def per_device(mesh, inputs, cotangent, gate_pre, up_pre, w_gate, w_up, w_down):
    rows, cols = mesh
    groups, lines = rows // 2, cols // 2

    def twin(x, axis, size):
        return lax.ppermute(x, axis, [(i, i ^ 1) for i in range(size)])

    def shift(x, axis, size, k):
        return lax.ppermute(x, axis, [(i, (i + 2 * k) % size) for i in range(size)])

    gates = [gate_pre] + [shift(gate_pre, "row", rows, -j) for j in range(1, groups)]
    ups = [up_pre] + [shift(up_pre, "row", rows, -j) for j in range(1, groups)]
    cot = [cotangent] + [shift(cotangent, "col", cols, k) for k in range(1, lines)]
    gate_f, up_f = jnp.stack(gates).astype(F32), jnp.stack(ups).astype(F32)
    sig = jax.nn.sigmoid(gate_f)
    act = gate_f * sig
    hid = (act * up_f).astype(BF16)
    slope = up_f * sig * (1.0 + gate_f * (1.0 - sig))
    cot[1], hid, slope, act = lax.optimization_barrier((cot[1], hid, slope, act))
    cot += [twin(b, "col", cols) for b in cot]
    hid = [hid, twin(hid, "row", rows)]

    blocks, sums, moving = cot, [], []
    for h in range(PARTS):
        mine, theirs, cot_all = hidden_grad(mesh, blocks, w_down, h, PARTS)
        blocks = [cot_all]
        if h == 0:
            mine, theirs, x_late = lax.optimization_barrier((mine, theirs, inputs))
            xs = [x_late] + [shift(x_late, "col", cols, k) for k in range(1, lines)]
        mine = mine + twin(theirs, "row", rows)
        sent = mine.astype(BF16)
        moving.append([shift(sent, "row", rows, k) for k in range(1, groups)])
        sums.append(mine)
    scale = 1.0 / math.sqrt(cot_all.shape[0])
    grad_down = outer(mesh, hid, True, cot_all, scale)
    xs += [twin(b, "col", cols) for b in xs]
    xs = [b[None] for b in xs]

    gate_grads, up_grads = [], []
    width = gate_pre.shape[1] // PARTS
    for h in range(PARTS):
        total = sums[h]
        for k, got in enumerate(moving[h], 1):
            got = got.astype(F32)
            total = total + jnp.stack([got[(j + k) % groups] for j in range(groups)])
        at = slice(h * width, (h + 1) * width)
        gate_grad = (total * slope[:, :, at]).astype(BF16)
        up_grad = (total * act[:, :, at]).astype(BF16)
        gate_grads += [gate_grad, twin(gate_grad, "row", rows)]
        up_grads += [up_grad, twin(up_grad, "row", rows)]

    results = []
    for h in range(PARTS):
        send, keep, gate_all, up_all = input_grad(
            mesh, gate_grads, up_grads, w_gate, w_up, h, PARTS
        )
        gate_grads, up_grads = [gate_all], [up_all]
        keep = keep + twin(send, "col", cols).astype(F32)
        out = keep[0]
        for k in range(1, lines):
            out = out + shift(keep[k].astype(BF16), "col", cols, k).astype(F32)
        results.append(out.astype(BF16))
    grad_gate = outer(mesh, xs, False, gate_all, scale)
    grad_up = outer(mesh, xs, False, up_all, scale)
    return (jnp.concatenate(results, axis=1), grad_gate, grad_up, grad_down)


def solution(mesh):
    sizes = (mesh.shape["row"], mesh.shape["col"])
    in_specs = (
        P("col", "row"),
        P("col", "row"),
        P("row", "col"),
        P("row", "col"),
        P("row", "col"),
        P("row", "col"),
        P("col", "row"),
    )
    out_specs = (P("col", "row"), P("row", "col"), P("row", "col"), P("col", "row"))

    def body(*args):
        return per_device(sizes, *args)

    return jax.shard_map(body, mesh=mesh, in_specs=in_specs, out_specs=out_specs, check_vma=False)
```

time: 341 us -> 183 us (0.54)
  waiting for transfers between devices: 222 us -> 64.3 us
  Pallas kernels: 0 us -> 67.6 us
  matrix products: 63.2 us -> 0 us
  starting transfers between devices: 0.45 us -> 36.9 us
  local copies, waits for them, and re-layouts: 35.6 us -> 3.03 us
  between operations: 14.1 us -> 0.87 us
  other arithmetic: 4.69 us -> 8.89 us
    all_gather x5 -> x0, waiting for transfers between devices: 128 us -> none  [the longest x1 54 us: per_device(): lax.all_gather(cotangent, 'col', axis=0, tiled=True)]
    reduce_scatter x2 -> x0, waiting for transfers between devices: 91.6 us -> none  [the longest x1 48.4 us: per_device(): lax.psum_scatter(contract_last(gate_grad_all, w_gate) + contract_last(up_...]
    pallas_call x0 -> x7, Pallas kernels: none -> 67.6 us  [call(): pl.pallas_call(body, grid=(steps,), in_specs=in_specs, out_specs=out_spec...]
    ppermute x0 -> x33, waiting for transfers between devices: none -> 64.3 us  [the longest x16 54.1 us: shift(): return lax.ppermute(x, axis, [(i, (i + 2 * k) % size) for i in range(size)])]
    dot_general x6 -> x0, matrix products: 63.2 us -> none  [the longest x3 32.8 us: contract_last(): lax.dot_general(left, right, (((1,), (1,)), ((), ())), preferred_element_...]
    ppermute x0 -> x33, starting transfers between devices: none -> 36.9 us  [the longest x16 23.8 us: shift(): return lax.ppermute(x, axis, [(i, (i + 2 * k) % size) for i in range(size)])]
    unnamed x12 -> x50, local copies, waits for them, and re-layouts: 35.6 us -> 2.77 us
    mul x0 -> x1, other arithmetic: none -> 3.7 us  [per_device(): slope = up_f * sig * (1.0 + gate_f * (1.0 - sig))]
  transfers between devices with their start and end apart: 7 -> 33, of which waited for: 6 -> 10; matrix products, arithmetic and copies ran while one was open for 26% -> 5% of each run, Pallas kernels for 0% -> 33%
where the time goes in v1:
time: 183 us; the launch traced here: 181 us
  Pallas kernels  67.6 us (37%)
  waiting for transfers between devices  64.3 us (35%)
  starting transfers between devices  36.9 us (20%)
  other arithmetic  8.89 us (5%)
  local copies, waits for them, and re-layouts  3.03 us (2%)
    pallas_call x7, Pallas kernels, call(): pl.pallas_call(body, grid=(steps,), in_specs=in_specs, out_specs=out_spec...  67.6 us
    ppermute x16, waiting for transfers between devices, shift(): return lax.ppermute(x, axis, [(i, (i + 2 * k) % size) for i in range(size)])  54.1 us
    ppermute x16, starting transfers between devices, shift(): return lax.ppermute(x, axis, [(i, (i + 2 * k) % size) for i in range(size)])  23.8 us
    ppermute x17, starting transfers between devices, twin(): return lax.ppermute(x, axis, [(i, i ^ 1) for i in range(size)])  13.1 us
    ppermute x17, waiting for transfers between devices, twin(): return lax.ppermute(x, axis, [(i, i ^ 1) for i in range(size)])  10.1 us
    mul x1, other arithmetic, per_device(): slope = up_f * sig * (1.0 + gate_f * (1.0 - sig))  3.7 us
  transfers between devices with their start and end apart: 33, of which 10 were waited for; matrix products, arithmetic and copies ran while one was open for 5% of the time, Pallas kernels for 33%

profile of v1, /device:TPU:0, one launch (start us, length us, event | category | flops | bytes accessed | tf_op | source)
XLA Modules:
  0.0 181.5 jit_solution(12187641843874624107)
XLA Ops:
  0.6 3.0 %collective-permute-start.1 = (bf16[128,2048]{1,0:T(8,128)(2,1)}, bf16[128,2048]{1,0:T(8,128)(2,1)S(1)}, u32[]{:S(2)}, u32[]{:S(2)}) collective-permute-start(bf16[128,2048]{1,0:T(8,128)(2,1)} %param.9), channel_id=1, source_target_pairs={{0,16},{8,24},{16,0},{24,8},{1,17},{9,25},{17,1},{25,9},{2,18},{10... | collective-permute-start | bytes 1572872 | tf_op jit(solution)/shard_map/ppermute | solution.py:189
  3.7 4.1 %collective-permute-start.4 = (bf16[64,2048]{1,0:T(8,128)(2,1)}, bf16[64,2048]{1,0:T(8,128)(2,1)S(1)}, u32[]{:S(2)}, u32[]{:S(2)}) collective-permute-start(bf16[64,2048]{1,0:T(8,128)(2,1)} %refs_0_.1), channel_id=1, source_target_pairs={{0,6},{1,7},{2,0},{3,1},{4,2},{5,3},{6,4},{7,5},{8,14},{9,15},{10,... | collective-permute-start | bytes 786440 | tf_op jit(solution)/shard_map/ppermute | solution.py:189
  8.8 6.0 %collective-permute-done.4.refs_3_ = bf16[64,2048]{1,0:T(8,128)(2,1)S(1)} collective-permute-done((bf16[64,2048]{1,0:T(8,128)(2,1)}, bf16[64,2048]{1,0:T(8,128)(2,1)S(1)}, u32[]{:S(2)}, u32[]{:S(2)}) %collective-permute-start.4) | collective-permute-done | bytes 262176 | tf_op jit(solution)/shard_map/ppermute | solution.py:189
  16.4 13.4 %collective-permute-done.3.refs_2_ = bf16[64,2048]{1,0:T(8,128)(2,1)S(1)} collective-permute-done((bf16[64,2048]{1,0:T(8,128)(2,1)}, bf16[64,2048]{1,0:T(8,128)(2,1)S(1)}, u32[]{:S(2)}, u32[]{:S(2)}) %collective-permute-start.3) | collective-permute-done | bytes 262176 | tf_op jit(solution)/shard_map/ppermute | solution.py:189
  31.8 3.7 %fusion.1 = (f32[2,128,2048]{2,1,0:T(8,128)S(1)}, bf16[2,128,2048]{2,1,0:T(8,128)(2,1)S(1)}, f32[2,128,2048]{2,1,0:T(8,128)}) fusion(bf16[1,128,2048]{2,1,0:T(8,128)(2,1)S(1)} %bitcast.72, bf16[1,128,2048]{2,1,0:T(8,128)(2,1)} %bitcast.69, bf16[1,128,2048]{2,1,0:T(8,128)(2,1)S(1)} %bitcast.71, bf16[1,128,2048]{2,1,0:T(8,128)(2,1)} %bitcast.70), kind=kLoop, calls=%fused_computation.6 | loop fusion | flops 7864320 | bytes 7340032 | tf_op jit(solution)/shard_map/mul | solution.py:198
  37.1 1.8 %collective-permute-done.8.refs_7_ = bf16[64,2048]{1,0:T(8,128)(2,1)S(1)} collective-permute-done((bf16[64,2048]{1,0:T(8,128)(2,1)S(1)}, bf16[64,2048]{1,0:T(8,128)(2,1)S(1)}, u32[]{:S(2)}, u32[]{:S(2)}) %collective-permute-start.8) | collective-permute-done | bytes 262176 | tf_op jit(solution)/shard_map/ppermute | solution.py:186
  38.9 5.6 %collective-permute-done.7.refs_6_ = bf16[64,2048]{1,0:T(8,128)(2,1)S(1)} collective-permute-done((bf16[64,2048]{1,0:T(8,128)(2,1)S(1)}, bf16[64,2048]{1,0:T(8,128)(2,1)S(1)}, u32[]{:S(2)}, u32[]{:S(2)}) %collective-permute-start.7) | collective-permute-done | bytes 262176 | tf_op jit(solution)/shard_map/ppermute | solution.py:186
  45.3 2.5 %collective-permute-done.6.refs_5_ = bf16[64,2048]{1,0:T(8,128)(2,1)} collective-permute-done((bf16[64,2048]{1,0:T(8,128)(2,1)S(1)}, bf16[64,2048]{1,0:T(8,128)(2,1)}, u32[]{:S(2)}, u32[]{:S(2)}) %collective-permute-start.6) | collective-permute-done | bytes 262176 | tf_op jit(solution)/shard_map/ppermute | solution.py:186
  47.7 7.1 %shard_map.102 = (f32[2,128,1024]{2,1,0:T(8,128)}, f32[2,128,1024]{2,1,0:T(8,128)}, bf16[8,64,2048]{2,1,0:T(8,128)(2,1)}) custom-call(bf16[64,2048]{1,0:T(8,128)(2,1)} %refs_0_.1, bf16[64,2048]{1,0:T(8,128)(2,1)} %copy-done.21, bf16[64,2048]{1,0:T(8,128)(2,1)} %copy-done.20, bf16[64,2048]{1,0:T(8,128)(2,1)} %copy-done.19, bf16[64,2048]{1,0:T(8,128)(2,1)} %copy-done.22, ...), custom_call_target="tpu_custom_call" | custom-call | flops 2147483648 | bytes 14680064 | tf_op jit(solution)/shard_map/pallas_call | solution.py:29
  54.8 6.7 %shard_map.103 = (f32[2,128,1024]{2,1,0:T(8,128)}, f32[2,128,1024]{2,1,0:T(8,128)}) custom-call(bf16[512,2048]{1,0:T(8,128)(2,1)} %bitcast.47, bf16[2048,2048]{1,0:T(8,128)(2,1)} %refs_1_.1), custom_call_target="tpu_custom_call" | custom-call | flops 2147483648 | bytes 12582912 | tf_op jit(solution)/shard_map/pallas_call | solution.py:29
  67.6 11.0 %collective-permute-done.10 = bf16[2,128,1024]{2,1,0:T(8,128)(2,1)S(1)} collective-permute-done((bf16[2,128,1024]{2,1,0:T(8,128)(2,1)S(1)}, bf16[2,128,1024]{2,1,0:T(8,128)(2,1)S(1)}, u32[]{:S(2)}, u32[]{:S(2)}) %collective-permute-start.10) | collective-permute-done | bytes 524320 | tf_op jit(solution)/shard_map/ppermute | solution.py:189
  78.7 10.3 %collective-permute-done.13 = bf16[2,128,1024]{2,1,0:T(8,128)(2,1)S(1)} collective-permute-done((bf16[2,128,1024]{2,1,0:T(8,128)(2,1)S(1)}, bf16[2,128,1024]{2,1,0:T(8,128)(2,1)S(1)}, u32[]{:S(2)}, u32[]{:S(2)}) %collective-permute-start.13) | collective-permute-done | bytes 524320 | tf_op jit(solution)/shard_map/ppermute | solution.py:189
  89.1 2.0 %multiply_convert_fusion = (bf16[2,128,1024]{2,1,0:T(8,128)(2,1)S(1)}, bf16[2,128,1024]{2,1,0:T(8,128)(2,1)}, bf16[2,128,1024]{2,1,0:T(8,128)(2,1)}, bf16[2,128,1024]{2,1,0:T(8,128)(2,1)}) fusion(f32[2,128,2048]{2,1,0:T(8,128)S(1)} %copy-done, f32[2,128,1024]{2,1,0:T(8,128)S(1)} %get-tuple-element.45, f32[1,128,1024]{2,1,0:T(8,128)S(1)} %get-tuple-element.62, ...), kind=kLoop, calls=%fused_computation.17 | loop fusion | flops 3145728 | bytes 10485760 | tf_op jit(solution)/shard_map/convert_element_type | solution.py:228
  93.4 11.5 %shard_map.108 = f32[2048,2048]{1,0:T(8,128)} custom-call(bf16[2,128,2048]{2,1,0:T(8,128)(2,1)} %copy-done.1, bf16[2,128,2048]{2,1,0:T(8,128)(2,1)} %copy-done.13, bf16[512,2048]{1,0:T(8,128)(2,1)} %bitcast.48), custom_call_target="tpu_custom_call" | custom-call | flops 4294967296 | bytes 20971520 | tf_op jit(solution)/shard_map/pallas_call | solution.py:29
  109.2 10.0 %shard_map.104 = (bf16[4,64,1024]{2,1,0:T(8,128)(2,1)}, f32[4,64,1024]{2,1,0:T(8,128)}, bf16[4,128,2048]{2,1,0:T(8,128)(2,1)}, bf16[4,128,2048]{2,1,0:T(8,128)(2,1)}) custom-call(bf16[2,128,1024]{2,1,0:T(8,128)(2,1)} %get-tuple-element.50.refs_0_, bf16[2,128,1024]{2,1,0:T(8,128)(2,1)} %collective-permute-done.11.refs_1_, ...), custom_call_target="tpu_custom_call" | custom-call | flops 4294967296 | bytes 26738688 | tf_op jit(solution)/shard_map/pallas_call | solution.py:29
  120.8 9.4 %shard_map.105 = (bf16[4,64,1024]{2,1,0:T(8,128)(2,1)}, f32[4,64,1024]{2,1,0:T(8,128)}) custom-call(bf16[512,2048]{1,0:T(8,128)(2,1)} %bitcast.49, bf16[512,2048]{1,0:T(8,128)(2,1)} %bitcast.51, bf16[2048,2048]{1,0:T(8,128)(2,1)} %refs_2_.1, bf16[2048,2048]{1,0:T(8,128)(2,1)} %refs_3_.1), custom_call_target="tpu_custom_call" | custom-call | flops 4294967296 | bytes 22544384 | tf_op jit(solution)/shard_map/pallas_call | solution.py:29
  131.7 11.4 %shard_map.107 = f32[2048,2048]{1,0:T(8,128)} custom-call(bf16[1,64,2048]{2,1,0:T(8,128)(2,1)} %bitcast.53, bf16[1,64,2048]{2,1,0:T(8,128)(2,1)} %bitcast.59, bf16[1,64,2048]{2,1,0:T(8,128)(2,1)} %bitcast.57, bf16[1,64,2048]{2,1,0:T(8,128)(2,1)} %bitcast.55, bf16[1,64,2048]{2,1,0:T(8,128)(2,1)} %bitcast.61, bf16[1,64,2048]{2,1,0:T(8,128)(2,1)} %bitcast.67, ...), custom_call_target="tpu_custom_call" | custom-call | flops 4294967296 | bytes 20971520 | tf_op jit(solution)/shard_map/pallas_call | solution.py:29
  143.1 11.5 %shard_map.106 = f32[2048,2048]{1,0:T(8,128)} custom-call(bf16[1,64,2048]{2,1,0:T(8,128)(2,1)} %bitcast.54, bf16[1,64,2048]{2,1,0:T(8,128)(2,1)} %bitcast.60, bf16[1,64,2048]{2,1,0:T(8,128)(2,1)} %bitcast.58, bf16[1,64,2048]{2,1,0:T(8,128)(2,1)} %bitcast.56, bf16[1,64,2048]{2,1,0:T(8,128)(2,1)} %bitcast.62, bf16[1,64,2048]{2,1,0:T(8,128)(2,1)} %bitcast.68, ...), custom_call_target="tpu_custom_call" | custom-call | flops 4294967296 | bytes 20971520 | tf_op jit(solution)/shard_map/pallas_call | solution.py:29
  156.6 2.2 %collective-permute-start.20 = (bf16[64,1024]{1,0:T(8,128)(2,1)S(1)}, bf16[64,1024]{1,0:T(8,128)(2,1)S(1)}, u32[]{:S(2)}, u32[]{:S(2)}) collective-permute-start(bf16[64,1024]{1,0:T(8,128)(2,1)S(1)} %get-tuple-element.56), channel_id=1, source_target_pairs={{0,6},{1,7},{2,0},{3,1},{4,2},{5,3},{6,4},{7,5},{8,14},{9,15},{10,... | collective-permute-start | bytes 393224 | tf_op jit(solution)/shard_map/ppermute | solution.py:189
  159.6 2.1 %collective-permute-start.22 = (bf16[64,1024]{1,0:T(8,128)(2,1)S(1)}, bf16[64,1024]{1,0:T(8,128)(2,1)S(1)}, u32[]{:S(2)}, u32[]{:S(2)}) collective-permute-start(bf16[64,1024]{1,0:T(8,128)(2,1)S(1)} %get-tuple-element.58), channel_id=1, source_target_pairs={{0,2},{1,3},{2,4},{3,5},{4,6},{5,7},{6,0},{7,1},{8,10},{9,11},{10,... | collective-permute-start | bytes 393224 | tf_op jit(solution)/shard_map/ppermute | solution.py:189
  161.6 1.8 collective-permute-start.24
  163.4 3.8 %collective-permute-start.23 = (bf16[64,1024]{1,0:T(8,128)(2,1)S(1)}, bf16[64,1024]{1,0:T(8,128)(2,1)S(1)}, u32[]{:S(2)}, u32[]{:S(2)}) collective-permute-start(bf16[64,1024]{1,0:T(8,128)(2,1)S(1)} %get-tuple-element.60), channel_id=1, source_target_pairs={{0,4},{1,5},{2,6},{3,7},{4,0},{5,1},{6,2},{7,3},{8,12},{9,13},{10,... | collective-permute-start | bytes 393224 | tf_op jit(solution)/shard_map/ppermute | solution.py:189
  167.2 8.8 %collective-permute-done.19 = bf16[64,1024]{1,0:T(8,128)(2,1)S(1)} collective-permute-done((bf16[64,1024]{1,0:T(8,128)(2,1)S(1)}, bf16[64,1024]{1,0:T(8,128)(2,1)S(1)}, u32[]{:S(2)}, u32[]{:S(2)}) %collective-permute-start.19) | collective-permute-done | bytes 131104 | tf_op jit(solution)/shard_map/ppermute | solution.py:189
  176.1 4.6 %collective-permute-done.23 = bf16[64,1024]{1,0:T(8,128)(2,1)S(1)} collective-permute-done((bf16[64,1024]{1,0:T(8,128)(2,1)S(1)}, bf16[64,1024]{1,0:T(8,128)(2,1)S(1)}, u32[]{:S(2)}, u32[]{:S(2)}) %collective-permute-start.23) | collective-permute-done | bytes 131104 | tf_op jit(solution)/shard_map/ppermute | solution.py:189
  (112 shorter events, 26.5 us)
Async XLA Ops:
  0.6 30.7 %collective-permute-start.1 = (bf16[128,2048]{1,0:T(8,128)(2,1)}, bf16[128,2048]{1,0:T(8,128)(2,1)S(1)}, u32[]{:S(2)}, u32[]{:S(2)}) collective-permute-start(bf16[128,2048]{1,0:T(8,128)(2,1)} %param.9), channel_id=1, source_target_pairs={{0,16},{8,24},{16,0},{24,8},{1,17},{9,25},{17,1},{25,9},{2,18},{10... | collective-permute-start | bytes 1572872 | tf_op jit(solution)/shard_map/ppermute | solution.py:189
  3.7 28.1 %collective-permute-start.2 = (bf16[128,2048]{1,0:T(8,128)(2,1)}, bf16[128,2048]{1,0:T(8,128)(2,1)S(1)}, u32[]{:S(2)}, u32[]{:S(2)}) collective-permute-start(bf16[128,2048]{1,0:T(8,128)(2,1)} %param.10), channel_id=1, source_target_pairs={{0,16},{8,24},{16,0},{24,8},{1,17},{9,25},{17,1},{25,9},{2,18},{10... | collective-permute-start | bytes 1572872 | tf_op jit(solution)/shard_map/ppermute | solution.py:189
  7.8 22.0 %collective-permute-start.3 = (bf16[64,2048]{1,0:T(8,128)(2,1)}, bf16[64,2048]{1,0:T(8,128)(2,1)S(1)}, u32[]{:S(2)}, u32[]{:S(2)}) collective-permute-start(bf16[64,2048]{1,0:T(8,128)(2,1)} %refs_0_.1), channel_id=1, source_target_pairs={{0,4},{1,5},{2,6},{3,7},{4,0},{5,1},{6,2},{7,3},{8,12},{9,13},{10,... | collective-permute-start | bytes 786440 | tf_op jit(solution)/shard_map/ppermute | solution.py:189
  7.8 27.7 %collective-permute-start = (bf16[64,2048]{1,0:T(8,128)(2,1)}, bf16[64,2048]{1,0:T(8,128)(2,1)S(1)}, u32[]{:S(2)}, u32[]{:S(2)}) collective-permute-start(bf16[64,2048]{1,0:T(8,128)(2,1)} %refs_0_.1), channel_id=1, source_target_pairs={{0,2},{1,3},{2,4},{3,5},{4,6},{5,7},{6,0},{7,1},{8,10},{9,11},{10,... | collective-permute-start | bytes 786440 | tf_op jit(solution)/shard_map/ppermute | solution.py:189
  14.9 22.3 %collective-permute-start.5 = (bf16[64,2048]{1,0:T(8,128)(2,1)}, bf16[64,2048]{1,0:T(8,128)(2,1)S(1)}, u32[]{:S(2)}, u32[]{:S(2)}) collective-permute-start(bf16[64,2048]{1,0:T(8,128)(2,1)} %refs_0_.1), channel_id=1, source_target_pairs={{0,1},{1,0},{2,3},{3,2},{4,5},{5,4},{6,7},{7,6},{8,9},{9,8},{10,11... | collective-permute-start | bytes 786440 | tf_op jit(solution)/shard_map/ppermute | solution.py:186
  63.7 14.9 %collective-permute-start.10 = (bf16[2,128,1024]{2,1,0:T(8,128)(2,1)S(1)}, bf16[2,128,1024]{2,1,0:T(8,128)(2,1)S(1)}, u32[]{:S(2)}, u32[]{:S(2)}) collective-permute-start(bf16[2,128,1024]{2,1,0:T(8,128)(2,1)S(1)} %get-tuple-element.46), channel_id=1, source_target_pairs={{0,16},{8,24},{16,0},{24,8},{1,17},{9,25},{17,1},{25,9},{2,18},{10... | collective-permute-start | bytes 1572872 | tf_op jit(solution)/shard_map/ppermute | solution.py:189
  65.6 23.4 %collective-permute-start.13 = (bf16[2,128,1024]{2,1,0:T(8,128)(2,1)S(1)}, bf16[2,128,1024]{2,1,0:T(8,128)(2,1)S(1)}, u32[]{:S(2)}, u32[]{:S(2)}) collective-permute-start(bf16[2,128,1024]{2,1,0:T(8,128)(2,1)S(1)} %get-tuple-element.44), channel_id=1, source_target_pairs={{0,16},{8,24},{16,0},{24,8},{1,17},{9,25},{17,1},{25,9},{2,18},{10... | collective-permute-start | bytes 1572872 | tf_op jit(solution)/shard_map/ppermute | solution.py:189
  66.3 25.8 %collective-permute-start.32 = (bf16[2,128,2048]{2,1,0:T(8,128)(2,1)S(1)}, bf16[2,128,2048]{2,1,0:T(8,128)(2,1)S(1)}, u32[]{:S(2)}, u32[]{:S(2)}) collective-permute-start(bf16[2,128,2048]{2,1,0:T(8,128)(2,1)S(1)} %get-tuple-element.39.refs_0_), channel_id=1, source_target_pairs={{0,8},{8,0},{16,24},{24,16},{1,9},{9,1},{17,25},{25,17},{2,10},{10... | collective-permute-start | bytes 3145736 | tf_op jit(solution)/shard_map/ppermute | solution.py:186
  66.4 25.2 %collective-permute-start.27 = (bf16[64,2048]{1,0:T(8,128)(2,1)S(1)}, bf16[64,2048]{1,0:T(8,128)(2,1)S(1)}, u32[]{:S(2)}, u32[]{:S(2)}) collective-permute-start(bf16[64,2048]{1,0:T(8,128)(2,1)S(1)} %copy-done.3), channel_id=1, source_target_pairs={{0,6},{1,7},{2,0},{3,1},{4,2},{5,3},{6,4},{7,5},{8,14},{9,15},{10,... | collective-permute-start | bytes 786440 | tf_op jit(solution)/shard_map/ppermute | solution.py:189
  66.4 25.3 %collective-permute-start.26 = (bf16[64,2048]{1,0:T(8,128)(2,1)S(1)}, bf16[64,2048]{1,0:T(8,128)(2,1)S(1)}, u32[]{:S(2)}, u32[]{:S(2)}) collective-permute-start(bf16[64,2048]{1,0:T(8,128)(2,1)S(1)} %copy-done.3), channel_id=1, source_target_pairs={{0,4},{1,5},{2,6},{3,7},{4,0},{5,1},{6,2},{7,3},{8,12},{9,13},{10,... | collective-permute-start | bytes 786440 | tf_op jit(solution)/shard_map/ppermute | solution.py:189
  91.1 15.4 %collective-permute-start.16 = (bf16[2,128,1024]{2,1,0:T(8,128)(2,1)S(1)}, bf16[2,128,1024]{2,1,0:T(8,128)(2,1)S(1)}, u32[]{:S(2)}, u32[]{:S(2)}) collective-permute-start(bf16[2,128,1024]{2,1,0:T(8,128)(2,1)S(1)} %get-tuple-element.48.refs_6_), channel_id=1, source_target_pairs={{0,8},{8,0},{16,24},{24,16},{1,9},{9,1},{17,25},{25,17},{2,10},{10... | collective-permute-start | bytes 1572872 | tf_op jit(solution)/shard_map/ppermute | solution.py:186
  91.1 16.0 %collective-permute-start.14 = (bf16[2,128,1024]{2,1,0:T(8,128)(2,1)}, bf16[2,128,1024]{2,1,0:T(8,128)(2,1)S(1)}, u32[]{:S(2)}, u32[]{:S(2)}) collective-permute-start(bf16[2,128,1024]{2,1,0:T(8,128)(2,1)} %get-tuple-element.49.refs_2_), channel_id=1, source_target_pairs={{0,8},{8,0},{16,24},{24,16},{1,9},{9,1},{17,25},{25,17},{2,10},{10... | collective-permute-start | bytes 1572872 | tf_op jit(solution)/shard_map/ppermute | solution.py:186
  91.6 17.0 %collective-permute-start.11 = (bf16[2,128,1024]{2,1,0:T(8,128)(2,1)}, bf16[2,128,1024]{2,1,0:T(8,128)(2,1)}, u32[]{:S(2)}, u32[]{:S(2)}) collective-permute-start(bf16[2,128,1024]{2,1,0:T(8,128)(2,1)} %get-tuple-element.50.refs_0_), channel_id=1, source_target_pairs={{0,8},{8,0},{16,24},{24,16},{1,9},{9,1},{17,25},{25,17},{2,10},{10... | collective-permute-start | bytes 1572872 | tf_op jit(solution)/shard_map/ppermute | solution.py:186
  91.7 17.5 %collective-permute-start.15 = (bf16[2,128,1024]{2,1,0:T(8,128)(2,1)}, bf16[2,128,1024]{2,1,0:T(8,128)(2,1)}, u32[]{:S(2)}, u32[]{:S(2)}) collective-permute-start(bf16[2,128,1024]{2,1,0:T(8,128)(2,1)} %get-tuple-element.51.refs_4_), channel_id=1, source_target_pairs={{0,8},{8,0},{16,24},{24,16},{1,9},{9,1},{17,25},{25,17},{2,10},{10... | collective-permute-start | bytes 1572872 | tf_op jit(solution)/shard_map/ppermute | solution.py:186
  104.9 25.3 %collective-permute-start.28 = (bf16[64,2048]{1,0:T(8,128)(2,1)S(1)}, bf16[64,2048]{1,0:T(8,128)(2,1)S(1)}, u32[]{:S(2)}, u32[]{:S(2)}) collective-permute-start(bf16[64,2048]{1,0:T(8,128)(2,1)S(1)} %copy-done.3), channel_id=1, source_target_pairs={{0,1},{1,0},{2,3},{3,2},{4,5},{5,4},{6,7},{7,6},{8,9},{9,8},{10,11... | collective-permute-start | bytes 786440 | tf_op jit(solution)/shard_map/ppermute | solution.py:186
  106.5 24.3 %collective-permute-start.31 = (bf16[64,2048]{1,0:T(8,128)(2,1)S(1)}, bf16[64,2048]{1,0:T(8,128)(2,1)S(1)}, u32[]{:S(2)}, u32[]{:S(2)}) collective-permute-start(bf16[64,2048]{1,0:T(8,128)(2,1)S(1)} %copy-done.5), channel_id=1, source_target_pairs={{0,1},{1,0},{2,3},{3,2},{4,5},{5,4},{6,7},{7,6},{8,9},{9,8},{10,11... | collective-permute-start | bytes 786440 | tf_op jit(solution)/shard_map/ppermute | solution.py:186
  107.1 23.7 %collective-permute-start.30 = (bf16[64,2048]{1,0:T(8,128)(2,1)S(1)}, bf16[64,2048]{1,0:T(8,128)(2,1)S(1)}, u32[]{:S(2)}, u32[]{:S(2)}) collective-permute-start(bf16[64,2048]{1,0:T(8,128)(2,1)S(1)} %copy-done.7), channel_id=1, source_target_pairs={{0,1},{1,0},{2,3},{3,2},{4,5},{5,4},{6,7},{7,6},{8,9},{9,8},{10,11... | collective-permute-start | bytes 786440 | tf_op jit(solution)/shard_map/ppermute | solution.py:186
  108.7 22.3 %collective-permute-start.29 = (bf16[64,2048]{1,0:T(8,128)(2,1)S(1)}, bf16[64,2048]{1,0:T(8,128)(2,1)S(1)}, u32[]{:S(2)}, u32[]{:S(2)}) collective-permute-start(bf16[64,2048]{1,0:T(8,128)(2,1)S(1)} %collective-permute-done.25), channel_id=1, source_target_pairs={{0,1},{1,0},{2,3},{3,2},{4,5},{5,4},{6,7},{7,6},{8,9},{9,8},{10,11... | collective-permute-start | bytes 786440 | tf_op jit(solution)/shard_map/ppermute | solution.py:186
  119.2 35.5 %collective-permute-start.17 = (bf16[4,64,1024]{2,1,0:T(8,128)(2,1)}, bf16[4,64,1024]{2,1,0:T(8,128)(2,1)S(1)}, u32[]{:S(2)}, u32[]{:S(2)}) collective-permute-start(bf16[4,64,1024]{2,1,0:T(8,128)(2,1)} %get-tuple-element.33), channel_id=1, source_target_pairs={{0,1},{1,0},{2,3},{3,2},{4,5},{5,4},{6,7},{7,6},{8,9},{9,8},{10,11... | collective-permute-start | bytes 1572872 | tf_op jit(solution)/shard_map/ppermute | solution.py:186
  130.2 29.1 %collective-permute-start.21 = (bf16[4,64,1024]{2,1,0:T(8,128)(2,1)}, bf16[4,64,1024]{2,1,0:T(8,128)(2,1)S(1)}, u32[]{:S(2)}, u32[]{:S(2)}) collective-permute-start(bf16[4,64,1024]{2,1,0:T(8,128)(2,1)} %get-tuple-element.37), channel_id=1, source_target_pairs={{0,1},{1,0},{2,3},{3,2},{4,5},{5,4},{6,7},{7,6},{8,9},{9,8},{10,11... | collective-permute-start | bytes 1572872 | tf_op jit(solution)/shard_map/ppermute | solution.py:186
  158.8 17.2 %collective-permute-start.19 = (bf16[64,1024]{1,0:T(8,128)(2,1)S(1)}, bf16[64,1024]{1,0:T(8,128)(2,1)S(1)}, u32[]{:S(2)}, u32[]{:S(2)}) collective-permute-start(bf16[64,1024]{1,0:T(8,128)(2,1)S(1)} %get-tuple-element.57), channel_id=1, source_target_pairs={{0,4},{1,5},{2,6},{3,7},{4,0},{5,1},{6,2},{7,3},{8,12},{9,13},{10,... | collective-permute-start | bytes 393224 | tf_op jit(solution)/shard_map/ppermute | solution.py:189
  159.6 16.5 %collective-permute-start.22 = (bf16[64,1024]{1,0:T(8,128)(2,1)S(1)}, bf16[64,1024]{1,0:T(8,128)(2,1)S(1)}, u32[]{:S(2)}, u32[]{:S(2)}) collective-permute-start(bf16[64,1024]{1,0:T(8,128)(2,1)S(1)} %get-tuple-element.58), channel_id=1, source_target_pairs={{0,2},{1,3},{2,4},{3,5},{4,6},{5,7},{6,0},{7,1},{8,10},{9,11},{10,... | collective-permute-start | bytes 393224 | tf_op jit(solution)/shard_map/ppermute | solution.py:189
  161.6 14.4 %collective-permute-start.24 = (bf16[64,1024]{1,0:T(8,128)(2,1)S(1)}, bf16[64,1024]{1,0:T(8,128)(2,1)S(1)}, u32[]{:S(2)}, u32[]{:S(2)}) collective-permute-start(bf16[64,1024]{1,0:T(8,128)(2,1)S(1)} %get-tuple-element.59), channel_id=1, source_target_pairs={{0,6},{1,7},{2,0},{3,1},{4,2},{5,3},{6,4},{7,5},{8,14},{9,15},{10,... | collective-permute-start | bytes 393224 | tf_op jit(solution)/shard_map/ppermute | solution.py:189
  163.4 17.3 %collective-permute-start.23 = (bf16[64,1024]{1,0:T(8,128)(2,1)S(1)}, bf16[64,1024]{1,0:T(8,128)(2,1)S(1)}, u32[]{:S(2)}, u32[]{:S(2)}) collective-permute-start(bf16[64,1024]{1,0:T(8,128)(2,1)S(1)} %get-tuple-element.60), channel_id=1, source_target_pairs={{0,4},{1,5},{2,6},{3,7},{4,0},{5,1},{6,2},{7,3},{8,12},{9,13},{10,... | collective-permute-start | bytes 393224 | tf_op jit(solution)/shard_map/ppermute | solution.py:189
  (34 other events, 281.8 us)

commit v2 on v1

--- a/solution.py
+++ b/solution.py
@@ -149,7 +149,7 @@
     rows, cols = mesh
     tokens, wide = right.shape
     count, spread = len(left), left[0].shape[-1]
-    tile, size = tile_of(spread, 256), left[0].shape[1]
+    tile, size = tile_of(spread, 512), left[0].shape[1]
     every = sum(a.shape[0] for a in left)
 
     def body(*refs):
@@ -198,15 +198,14 @@
     slope = up_f * sig * (1.0 + gate_f * (1.0 - sig))
     cot[1], hid, slope, act = lax.optimization_barrier((cot[1], hid, slope, act))
     cot += [twin(b, "col", cols) for b in cot]
+    cot[-2], x_late = lax.optimization_barrier((cot[-2], inputs))
+    xs = [x_late] + [shift(x_late, "col", cols, k) for k in range(1, lines)]
     hid = [hid, twin(hid, "row", rows)]
 
     blocks, sums, moving = cot, [], []
     for h in range(PARTS):
         mine, theirs, cot_all = hidden_grad(mesh, blocks, w_down, h, PARTS)
         blocks = [cot_all]
-        if h == 0:
-            mine, theirs, x_late = lax.optimization_barrier((mine, theirs, inputs))
-            xs = [x_late] + [shift(x_late, "col", cols, k) for k in range(1, lines)]
         mine = mine + twin(theirs, "row", rows)
         sent = mine.astype(BF16)
         moving.append([shift(sent, "row", rows, k) for k in range(1, groups)])

time: 183 us -> 178 us (0.973)
  Pallas kernels: 67.6 us -> 64 us
    pallas_call x7, Pallas kernels: 67.6 us -> 64 us  [call(): pl.pallas_call(body, grid=(steps,), in_specs=in_specs, out_specs=out_spec...]
  transfers between devices with their start and end apart: 33 -> 33, of which waited for: 10 -> 11; matrix products, arithmetic and copies ran while one was open for 5% -> 5% of each run, Pallas kernels for 33% -> 32%
where the time goes in v2:
time: 178 us
  Pallas kernels  64 us (36%)
  waiting for transfers between devices  63.5 us (36%)
  starting transfers between devices  36.6 us (21%)
  other arithmetic  8.89 us (5%)
  local copies, waits for them, and re-layouts  3.81 us (2%)
    pallas_call x7, Pallas kernels, call(): pl.pallas_call(body, grid=(steps,), in_specs=in_specs, out_specs=out_spec...  64 us
    ppermute x16, waiting for transfers between devices, shift(): return lax.ppermute(x, axis, [(i, (i + 2 * k) % size) for i in range(size)])  54.1 us
    ppermute x16, starting transfers between devices, shift(): return lax.ppermute(x, axis, [(i, (i + 2 * k) % size) for i in range(size)])  23.6 us
    ppermute x17, starting transfers between devices, twin(): return lax.ppermute(x, axis, [(i, i ^ 1) for i in range(size)])  13.1 us
    ppermute x17, waiting for transfers between devices, twin(): return lax.ppermute(x, axis, [(i, i ^ 1) for i in range(size)])  9.34 us
    mul x1, other arithmetic, per_device(): slope = up_f * sig * (1.0 + gate_f * (1.0 - sig))  3.7 us
  transfers between devices with their start and end apart: 33, of which 11 were waited for; matrix products, arithmetic and copies ran while one was open for 5% of the time, Pallas kernels for 32%

profile of v2, /device:TPU:0, one launch (start us, length us, event | category | flops | bytes accessed | tf_op | source)
XLA Modules:
  0.0 177.6 jit_solution(8872702020440060968)
XLA Ops:
  0.6 3.0 %collective-permute-start.1 = (bf16[128,2048]{1,0:T(8,128)(2,1)}, bf16[128,2048]{1,0:T(8,128)(2,1)S(1)}, u32[]{:S(2)}, u32[]{:S(2)}) collective-permute-start(bf16[128,2048]{1,0:T(8,128)(2,1)} %param.9), channel_id=1, source_target_pairs={{0,16},{8,24},{16,0},{24,8},{1,17},{9,25},{17,1},{25,9},{2,18},{10... | collective-permute-start | bytes 1572872 | tf_op jit(solution)/shard_map/ppermute | solution.py:189
  3.7 4.1 %collective-permute-start.4 = (bf16[64,2048]{1,0:T(8,128)(2,1)}, bf16[64,2048]{1,0:T(8,128)(2,1)S(1)}, u32[]{:S(2)}, u32[]{:S(2)}) collective-permute-start(bf16[64,2048]{1,0:T(8,128)(2,1)} %refs_0_.1), channel_id=1, source_target_pairs={{0,6},{1,7},{2,0},{3,1},{4,2},{5,3},{6,4},{7,5},{8,14},{9,15},{10,... | collective-permute-start | bytes 786440 | tf_op jit(solution)/shard_map/ppermute | solution.py:189
  8.8 6.0 %collective-permute-done.4.refs_3_ = bf16[64,2048]{1,0:T(8,128)(2,1)S(1)} collective-permute-done((bf16[64,2048]{1,0:T(8,128)(2,1)}, bf16[64,2048]{1,0:T(8,128)(2,1)S(1)}, u32[]{:S(2)}, u32[]{:S(2)}) %collective-permute-start.4) | collective-permute-done | bytes 262176 | tf_op jit(solution)/shard_map/ppermute | solution.py:189
  16.4 13.4 %collective-permute-done.3.refs_2_ = bf16[64,2048]{1,0:T(8,128)(2,1)S(1)} collective-permute-done((bf16[64,2048]{1,0:T(8,128)(2,1)}, bf16[64,2048]{1,0:T(8,128)(2,1)S(1)}, u32[]{:S(2)}, u32[]{:S(2)}) %collective-permute-start.3) | collective-permute-done | bytes 262176 | tf_op jit(solution)/shard_map/ppermute | solution.py:189
  31.8 3.7 %fusion.1 = (f32[2,128,2048]{2,1,0:T(8,128)S(1)}, bf16[2,128,2048]{2,1,0:T(8,128)(2,1)S(1)}, f32[2,128,2048]{2,1,0:T(8,128)}) fusion(bf16[1,128,2048]{2,1,0:T(8,128)(2,1)S(1)} %bitcast.72, bf16[1,128,2048]{2,1,0:T(8,128)(2,1)} %bitcast.69, bf16[1,128,2048]{2,1,0:T(8,128)(2,1)S(1)} %bitcast.71, bf16[1,128,2048]{2,1,0:T(8,128)(2,1)} %bitcast.70), kind=kLoop, calls=%fused_computation.6 | loop fusion | flops 7864320 | bytes 7340032 | tf_op jit(solution)/shard_map/mul | solution.py:198
  37.1 7.4 %collective-permute-done.7.refs_6_ = bf16[64,2048]{1,0:T(8,128)(2,1)S(1)} collective-permute-done((bf16[64,2048]{1,0:T(8,128)(2,1)S(1)}, bf16[64,2048]{1,0:T(8,128)(2,1)S(1)}, u32[]{:S(2)}, u32[]{:S(2)}) %collective-permute-start.7) | collective-permute-done | bytes 262176 | tf_op jit(solution)/shard_map/ppermute | solution.py:186
  46.1 1.7 collective-permute-done.6.refs_5_
  47.7 7.1 %shard_map.102 = (f32[2,128,1024]{2,1,0:T(8,128)}, f32[2,128,1024]{2,1,0:T(8,128)}, bf16[8,64,2048]{2,1,0:T(8,128)(2,1)}) custom-call(bf16[64,2048]{1,0:T(8,128)(2,1)} %refs_0_.1, bf16[64,2048]{1,0:T(8,128)(2,1)} %copy-done.21, bf16[64,2048]{1,0:T(8,128)(2,1)} %copy-done.20, bf16[64,2048]{1,0:T(8,128)(2,1)} %copy-done.19, bf16[64,2048]{1,0:T(8,128)(2,1)} %copy-done.22, ...), custom_call_target="tpu_custom_call" | custom-call | flops 2147483648 | bytes 14680064 | tf_op jit(solution)/shard_map/pallas_call | solution.py:29
  54.8 6.7 %shard_map.103 = (f32[2,128,1024]{2,1,0:T(8,128)}, f32[2,128,1024]{2,1,0:T(8,128)}) custom-call(bf16[512,2048]{1,0:T(8,128)(2,1)} %bitcast.47, bf16[2048,2048]{1,0:T(8,128)(2,1)} %refs_1_.1), custom_call_target="tpu_custom_call" | custom-call | flops 2147483648 | bytes 12582912 | tf_op jit(solution)/shard_map/pallas_call | solution.py:29
  62.0 1.7 fusion.17
  67.6 11.0 %collective-permute-done.10 = bf16[2,128,1024]{2,1,0:T(8,128)(2,1)S(1)} collective-permute-done((bf16[2,128,1024]{2,1,0:T(8,128)(2,1)S(1)}, bf16[2,128,1024]{2,1,0:T(8,128)(2,1)S(1)}, u32[]{:S(2)}, u32[]{:S(2)}) %collective-permute-start.10) | collective-permute-done | bytes 524320 | tf_op jit(solution)/shard_map/ppermute | solution.py:189
  78.7 10.3 %collective-permute-done.13 = bf16[2,128,1024]{2,1,0:T(8,128)(2,1)S(1)} collective-permute-done((bf16[2,128,1024]{2,1,0:T(8,128)(2,1)S(1)}, bf16[2,128,1024]{2,1,0:T(8,128)(2,1)S(1)}, u32[]{:S(2)}, u32[]{:S(2)}) %collective-permute-start.13) | collective-permute-done | bytes 524320 | tf_op jit(solution)/shard_map/ppermute | solution.py:189
  89.1 2.0 %multiply_convert_fusion = (bf16[2,128,1024]{2,1,0:T(8,128)(2,1)S(1)}, bf16[2,128,1024]{2,1,0:T(8,128)(2,1)}, bf16[2,128,1024]{2,1,0:T(8,128)(2,1)}, bf16[2,128,1024]{2,1,0:T(8,128)(2,1)}) fusion(f32[2,128,2048]{2,1,0:T(8,128)S(1)} %copy-done, f32[2,128,1024]{2,1,0:T(8,128)S(1)} %get-tuple-element.43, f32[1,128,1024]{2,1,0:T(8,128)S(1)} %get-tuple-element.60, ...), kind=kLoop, calls=%fused_computation.17 | loop fusion | flops 3145728 | bytes 10485760 | tf_op jit(solution)/shard_map/convert_element_type | solution.py:227
  93.4 10.0 %shard_map.108 = f32[2048,2048]{1,0:T(8,128)} custom-call(bf16[2,128,2048]{2,1,0:T(8,128)(2,1)} %copy-done.1, bf16[2,128,2048]{2,1,0:T(8,128)(2,1)} %copy-done.13, bf16[512,2048]{1,0:T(8,128)(2,1)} %bitcast.48), custom_call_target="tpu_custom_call" | custom-call | flops 4294967296 | bytes 20971520 | tf_op jit(solution)/shard_map/pallas_call | solution.py:29
  108.0 10.0 %shard_map.104 = (bf16[4,64,1024]{2,1,0:T(8,128)(2,1)}, f32[4,64,1024]{2,1,0:T(8,128)}, bf16[4,128,2048]{2,1,0:T(8,128)(2,1)}, bf16[4,128,2048]{2,1,0:T(8,128)(2,1)}) custom-call(bf16[2,128,1024]{2,1,0:T(8,128)(2,1)} %get-tuple-element.48.refs_0_, bf16[2,128,1024]{2,1,0:T(8,128)(2,1)} %collective-permute-done.11.refs_1_, ...), custom_call_target="tpu_custom_call" | custom-call | flops 4294967296 | bytes 26738688 | tf_op jit(solution)/shard_map/pallas_call | solution.py:29
  119.6 9.4 %shard_map.105 = (bf16[4,64,1024]{2,1,0:T(8,128)(2,1)}, f32[4,64,1024]{2,1,0:T(8,128)}) custom-call(bf16[512,2048]{1,0:T(8,128)(2,1)} %bitcast.49, bf16[512,2048]{1,0:T(8,128)(2,1)} %bitcast.51, bf16[2048,2048]{1,0:T(8,128)(2,1)} %refs_2_.1, bf16[2048,2048]{1,0:T(8,128)(2,1)} %refs_3_.1), custom_call_target="tpu_custom_call" | custom-call | flops 4294967296 | bytes 22544384 | tf_op jit(solution)/shard_map/pallas_call | solution.py:29
  130.6 10.3 %shard_map.107 = f32[2048,2048]{1,0:T(8,128)} custom-call(bf16[1,64,2048]{2,1,0:T(8,128)(2,1)} %bitcast.53, bf16[1,64,2048]{2,1,0:T(8,128)(2,1)} %bitcast.59, bf16[1,64,2048]{2,1,0:T(8,128)(2,1)} %bitcast.57, bf16[1,64,2048]{2,1,0:T(8,128)(2,1)} %bitcast.55, bf16[1,64,2048]{2,1,0:T(8,128)(2,1)} %bitcast.61, bf16[1,64,2048]{2,1,0:T(8,128)(2,1)} %bitcast.67, ...), custom_call_target="tpu_custom_call" | custom-call | flops 4294967296 | bytes 20971520 | tf_op jit(solution)/shard_map/pallas_call | solution.py:29
  140.9 10.4 %shard_map.106 = f32[2048,2048]{1,0:T(8,128)} custom-call(bf16[1,64,2048]{2,1,0:T(8,128)(2,1)} %bitcast.54, bf16[1,64,2048]{2,1,0:T(8,128)(2,1)} %bitcast.60, bf16[1,64,2048]{2,1,0:T(8,128)(2,1)} %bitcast.58, bf16[1,64,2048]{2,1,0:T(8,128)(2,1)} %bitcast.56, bf16[1,64,2048]{2,1,0:T(8,128)(2,1)} %bitcast.62, bf16[1,64,2048]{2,1,0:T(8,128)(2,1)} %bitcast.68, ...), custom_call_target="tpu_custom_call" | custom-call | flops 4294967296 | bytes 20971520 | tf_op jit(solution)/shard_map/pallas_call | solution.py:29
  153.0 2.4 %collective-permute-start.20 = (bf16[64,1024]{1,0:T(8,128)(2,1)S(1)}, bf16[64,1024]{1,0:T(8,128)(2,1)S(1)}, u32[]{:S(2)}, u32[]{:S(2)}) collective-permute-start(bf16[64,1024]{1,0:T(8,128)(2,1)S(1)} %get-tuple-element.54), channel_id=1, source_target_pairs={{0,6},{1,7},{2,0},{3,1},{4,2},{5,3},{6,4},{7,5},{8,14},{9,15},{10,... | collective-permute-start | bytes 393224 | tf_op jit(solution)/shard_map/ppermute | solution.py:189
  156.0 2.1 %collective-permute-start.22 = (bf16[64,1024]{1,0:T(8,128)(2,1)S(1)}, bf16[64,1024]{1,0:T(8,128)(2,1)S(1)}, u32[]{:S(2)}, u32[]{:S(2)}) collective-permute-start(bf16[64,1024]{1,0:T(8,128)(2,1)S(1)} %get-tuple-element.56), channel_id=1, source_target_pairs={{0,2},{1,3},{2,4},{3,5},{4,6},{5,7},{6,0},{7,1},{8,10},{9,11},{10,... | collective-permute-start | bytes 393224 | tf_op jit(solution)/shard_map/ppermute | solution.py:189
  158.0 1.8 %collective-permute-start.24 = (bf16[64,1024]{1,0:T(8,128)(2,1)S(1)}, bf16[64,1024]{1,0:T(8,128)(2,1)S(1)}, u32[]{:S(2)}, u32[]{:S(2)}) collective-permute-start(bf16[64,1024]{1,0:T(8,128)(2,1)S(1)} %get-tuple-element.57), channel_id=1, source_target_pairs={{0,6},{1,7},{2,0},{3,1},{4,2},{5,3},{6,4},{7,5},{8,14},{9,15},{10,... | collective-permute-start | bytes 393224 | tf_op jit(solution)/shard_map/ppermute | solution.py:189
  159.9 3.9 %collective-permute-start.23 = (bf16[64,1024]{1,0:T(8,128)(2,1)S(1)}, bf16[64,1024]{1,0:T(8,128)(2,1)S(1)}, u32[]{:S(2)}, u32[]{:S(2)}) collective-permute-start(bf16[64,1024]{1,0:T(8,128)(2,1)S(1)} %get-tuple-element.58), channel_id=1, source_target_pairs={{0,4},{1,5},{2,6},{3,7},{4,0},{5,1},{6,2},{7,3},{8,12},{9,13},{10,... | collective-permute-start | bytes 393224 | tf_op jit(solution)/shard_map/ppermute | solution.py:189
  163.8 8.8 %collective-permute-done.19 = bf16[64,1024]{1,0:T(8,128)(2,1)S(1)} collective-permute-done((bf16[64,1024]{1,0:T(8,128)(2,1)S(1)}, bf16[64,1024]{1,0:T(8,128)(2,1)S(1)}, u32[]{:S(2)}, u32[]{:S(2)}) %collective-permute-start.19) | collective-permute-done | bytes 131104 | tf_op jit(solution)/shard_map/ppermute | solution.py:189
  172.6 4.2 %collective-permute-done.23 = bf16[64,1024]{1,0:T(8,128)(2,1)S(1)} collective-permute-done((bf16[64,1024]{1,0:T(8,128)(2,1)S(1)}, bf16[64,1024]{1,0:T(8,128)(2,1)S(1)}, u32[]{:S(2)}, u32[]{:S(2)}) %collective-permute-start.23) | collective-permute-done | bytes 131104 | tf_op jit(solution)/shard_map/ppermute | solution.py:189
  (112 shorter events, 25.4 us)
Async XLA Ops:
  0.6 30.7 %collective-permute-start.1 = (bf16[128,2048]{1,0:T(8,128)(2,1)}, bf16[128,2048]{1,0:T(8,128)(2,1)S(1)}, u32[]{:S(2)}, u32[]{:S(2)}) collective-permute-start(bf16[128,2048]{1,0:T(8,128)(2,1)} %param.9), channel_id=1, source_target_pairs={{0,16},{8,24},{16,0},{24,8},{1,17},{9,25},{17,1},{25,9},{2,18},{10... | collective-permute-start | bytes 1572872 | tf_op jit(solution)/shard_map/ppermute | solution.py:189
  3.7 28.1 %collective-permute-start.2 = (bf16[128,2048]{1,0:T(8,128)(2,1)}, bf16[128,2048]{1,0:T(8,128)(2,1)S(1)}, u32[]{:S(2)}, u32[]{:S(2)}) collective-permute-start(bf16[128,2048]{1,0:T(8,128)(2,1)} %param.10), channel_id=1, source_target_pairs={{0,16},{8,24},{16,0},{24,8},{1,17},{9,25},{17,1},{25,9},{2,18},{10... | collective-permute-start | bytes 1572872 | tf_op jit(solution)/shard_map/ppermute | solution.py:189
  7.8 22.0 %collective-permute-start.3 = (bf16[64,2048]{1,0:T(8,128)(2,1)}, bf16[64,2048]{1,0:T(8,128)(2,1)S(1)}, u32[]{:S(2)}, u32[]{:S(2)}) collective-permute-start(bf16[64,2048]{1,0:T(8,128)(2,1)} %refs_0_.1), channel_id=1, source_target_pairs={{0,4},{1,5},{2,6},{3,7},{4,0},{5,1},{6,2},{7,3},{8,12},{9,13},{10,... | collective-permute-start | bytes 786440 | tf_op jit(solution)/shard_map/ppermute | solution.py:189
  7.8 27.7 %collective-permute-start = (bf16[64,2048]{1,0:T(8,128)(2,1)}, bf16[64,2048]{1,0:T(8,128)(2,1)S(1)}, u32[]{:S(2)}, u32[]{:S(2)}) collective-permute-start(bf16[64,2048]{1,0:T(8,128)(2,1)} %refs_0_.1), channel_id=1, source_target_pairs={{0,2},{1,3},{2,4},{3,5},{4,6},{5,7},{6,0},{7,1},{8,10},{9,11},{10,... | collective-permute-start | bytes 786440 | tf_op jit(solution)/shard_map/ppermute | solution.py:189
  14.9 29.7 %collective-permute-start.5 = (bf16[64,2048]{1,0:T(8,128)(2,1)}, bf16[64,2048]{1,0:T(8,128)(2,1)S(1)}, u32[]{:S(2)}, u32[]{:S(2)}) collective-permute-start(bf16[64,2048]{1,0:T(8,128)(2,1)} %refs_0_.1), channel_id=1, source_target_pairs={{0,1},{1,0},{2,3},{3,2},{4,5},{5,4},{6,7},{7,6},{8,9},{9,8},{10,11... | collective-permute-start | bytes 786440 | tf_op jit(solution)/shard_map/ppermute | solution.py:186
  29.8 14.8 %collective-permute-start.8 = (bf16[64,2048]{1,0:T(8,128)(2,1)S(1)}, bf16[64,2048]{1,0:T(8,128)(2,1)S(1)}, u32[]{:S(2)}, u32[]{:S(2)}) collective-permute-start(bf16[64,2048]{1,0:T(8,128)(2,1)S(1)} %collective-permute-done.4.refs_3_), channel_id=1, source_target_pairs={{0,1},{1,0},{2,3},{3,2},{4,5},{5,4},{6,7},{7,6},{8,9},{9,8},{10,11... | collective-permute-start | bytes 786440 | tf_op jit(solution)/shard_map/ppermute | solution.py:186
  63.8 14.9 %collective-permute-start.10 = (bf16[2,128,1024]{2,1,0:T(8,128)(2,1)S(1)}, bf16[2,128,1024]{2,1,0:T(8,128)(2,1)S(1)}, u32[]{:S(2)}, u32[]{:S(2)}) collective-permute-start(bf16[2,128,1024]{2,1,0:T(8,128)(2,1)S(1)} %get-tuple-element.44), channel_id=1, source_target_pairs={{0,16},{8,24},{16,0},{24,8},{1,17},{9,25},{17,1},{25,9},{2,18},{10... | collective-permute-start | bytes 1572872 | tf_op jit(solution)/shard_map/ppermute | solution.py:189
  65.6 23.4 %collective-permute-start.13 = (bf16[2,128,1024]{2,1,0:T(8,128)(2,1)S(1)}, bf16[2,128,1024]{2,1,0:T(8,128)(2,1)S(1)}, u32[]{:S(2)}, u32[]{:S(2)}) collective-permute-start(bf16[2,128,1024]{2,1,0:T(8,128)(2,1)S(1)} %get-tuple-element.42), channel_id=1, source_target_pairs={{0,16},{8,24},{16,0},{24,8},{1,17},{9,25},{17,1},{25,9},{2,18},{10... | collective-permute-start | bytes 1572872 | tf_op jit(solution)/shard_map/ppermute | solution.py:189
  66.3 25.8 %collective-permute-start.32 = (bf16[2,128,2048]{2,1,0:T(8,128)(2,1)S(1)}, bf16[2,128,2048]{2,1,0:T(8,128)(2,1)S(1)}, u32[]{:S(2)}, u32[]{:S(2)}) collective-permute-start(bf16[2,128,2048]{2,1,0:T(8,128)(2,1)S(1)} %get-tuple-element.37.refs_0_), channel_id=1, source_target_pairs={{0,8},{8,0},{16,24},{24,16},{1,9},{9,1},{17,25},{25,17},{2,10},{10... | collective-permute-start | bytes 3145736 | tf_op jit(solution)/shard_map/ppermute | solution.py:186
  66.4 25.2 %collective-permute-start.27 = (bf16[64,2048]{1,0:T(8,128)(2,1)S(1)}, bf16[64,2048]{1,0:T(8,128)(2,1)S(1)}, u32[]{:S(2)}, u32[]{:S(2)}) collective-permute-start(bf16[64,2048]{1,0:T(8,128)(2,1)S(1)} %copy-done.3), channel_id=1, source_target_pairs={{0,6},{1,7},{2,0},{3,1},{4,2},{5,3},{6,4},{7,5},{8,14},{9,15},{10,... | collective-permute-start | bytes 786440 | tf_op jit(solution)/shard_map/ppermute | solution.py:189
  66.4 25.3 %collective-permute-start.26 = (bf16[64,2048]{1,0:T(8,128)(2,1)S(1)}, bf16[64,2048]{1,0:T(8,128)(2,1)S(1)}, u32[]{:S(2)}, u32[]{:S(2)}) collective-permute-start(bf16[64,2048]{1,0:T(8,128)(2,1)S(1)} %copy-done.3), channel_id=1, source_target_pairs={{0,4},{1,5},{2,6},{3,7},{4,0},{5,1},{6,2},{7,3},{8,12},{9,13},{10,... | collective-permute-start | bytes 786440 | tf_op jit(solution)/shard_map/ppermute | solution.py:189
  91.1 14.8 %collective-permute-start.14 = (bf16[2,128,1024]{2,1,0:T(8,128)(2,1)}, bf16[2,128,1024]{2,1,0:T(8,128)(2,1)S(1)}, u32[]{:S(2)}, u32[]{:S(2)}) collective-permute-start(bf16[2,128,1024]{2,1,0:T(8,128)(2,1)} %get-tuple-element.47.refs_2_), channel_id=1, source_target_pairs={{0,8},{8,0},{16,24},{24,16},{1,9},{9,1},{17,25},{25,17},{2,10},{10... | collective-permute-start | bytes 1572872 | tf_op jit(solution)/shard_map/ppermute | solution.py:186
  91.6 15.9 %collective-permute-start.11 = (bf16[2,128,1024]{2,1,0:T(8,128)(2,1)}, bf16[2,128,1024]{2,1,0:T(8,128)(2,1)}, u32[]{:S(2)}, u32[]{:S(2)}) collective-permute-start(bf16[2,128,1024]{2,1,0:T(8,128)(2,1)} %get-tuple-element.48.refs_0_), channel_id=1, source_target_pairs={{0,8},{8,0},{16,24},{24,16},{1,9},{9,1},{17,25},{25,17},{2,10},{10... | collective-permute-start | bytes 1572872 | tf_op jit(solution)/shard_map/ppermute | solution.py:186
  91.7 16.3 %collective-permute-start.15 = (bf16[2,128,1024]{2,1,0:T(8,128)(2,1)}, bf16[2,128,1024]{2,1,0:T(8,128)(2,1)}, u32[]{:S(2)}, u32[]{:S(2)}) collective-permute-start(bf16[2,128,1024]{2,1,0:T(8,128)(2,1)} %get-tuple-element.49.refs_4_), channel_id=1, source_target_pairs={{0,8},{8,0},{16,24},{24,16},{1,9},{9,1},{17,25},{25,17},{2,10},{10... | collective-permute-start | bytes 1572872 | tf_op jit(solution)/shard_map/ppermute | solution.py:186
  103.8 25.2 %collective-permute-start.28 = (bf16[64,2048]{1,0:T(8,128)(2,1)S(1)}, bf16[64,2048]{1,0:T(8,128)(2,1)S(1)}, u32[]{:S(2)}, u32[]{:S(2)}) collective-permute-start(bf16[64,2048]{1,0:T(8,128)(2,1)S(1)} %copy-done.3), channel_id=1, source_target_pairs={{0,1},{1,0},{2,3},{3,2},{4,5},{5,4},{6,7},{7,6},{8,9},{9,8},{10,11... | collective-permute-start | bytes 786440 | tf_op jit(solution)/shard_map/ppermute | solution.py:186
  105.4 24.3 %collective-permute-start.31 = (bf16[64,2048]{1,0:T(8,128)(2,1)S(1)}, bf16[64,2048]{1,0:T(8,128)(2,1)S(1)}, u32[]{:S(2)}, u32[]{:S(2)}) collective-permute-start(bf16[64,2048]{1,0:T(8,128)(2,1)S(1)} %copy-done.5), channel_id=1, source_target_pairs={{0,1},{1,0},{2,3},{3,2},{4,5},{5,4},{6,7},{7,6},{8,9},{9,8},{10,11... | collective-permute-start | bytes 786440 | tf_op jit(solution)/shard_map/ppermute | solution.py:186
  105.9 23.7 %collective-permute-start.30 = (bf16[64,2048]{1,0:T(8,128)(2,1)S(1)}, bf16[64,2048]{1,0:T(8,128)(2,1)S(1)}, u32[]{:S(2)}, u32[]{:S(2)}) collective-permute-start(bf16[64,2048]{1,0:T(8,128)(2,1)S(1)} %copy-done.7), channel_id=1, source_target_pairs={{0,1},{1,0},{2,3},{3,2},{4,5},{5,4},{6,7},{7,6},{8,9},{9,8},{10,11... | collective-permute-start | bytes 786440 | tf_op jit(solution)/shard_map/ppermute | solution.py:186
  107.5 22.4 %collective-permute-start.29 = (bf16[64,2048]{1,0:T(8,128)(2,1)S(1)}, bf16[64,2048]{1,0:T(8,128)(2,1)S(1)}, u32[]{:S(2)}, u32[]{:S(2)}) collective-permute-start(bf16[64,2048]{1,0:T(8,128)(2,1)S(1)} %collective-permute-done.25), channel_id=1, source_target_pairs={{0,1},{1,0},{2,3},{3,2},{4,5},{5,4},{6,7},{7,6},{8,9},{9,8},{10,11... | collective-permute-start | bytes 786440 | tf_op jit(solution)/shard_map/ppermute | solution.py:186
  118.0 33.3 %collective-permute-start.17 = (bf16[4,64,1024]{2,1,0:T(8,128)(2,1)}, bf16[4,64,1024]{2,1,0:T(8,128)(2,1)S(1)}, u32[]{:S(2)}, u32[]{:S(2)}) collective-permute-start(bf16[4,64,1024]{2,1,0:T(8,128)(2,1)} %get-tuple-element.31), channel_id=1, source_target_pairs={{0,1},{1,0},{2,3},{3,2},{4,5},{5,4},{6,7},{7,6},{8,9},{9,8},{10,11... | collective-permute-start | bytes 1572872 | tf_op jit(solution)/shard_map/ppermute | solution.py:186
  129.1 26.6 %collective-permute-start.21 = (bf16[4,64,1024]{2,1,0:T(8,128)(2,1)}, bf16[4,64,1024]{2,1,0:T(8,128)(2,1)S(1)}, u32[]{:S(2)}, u32[]{:S(2)}) collective-permute-start(bf16[4,64,1024]{2,1,0:T(8,128)(2,1)} %get-tuple-element.35), channel_id=1, source_target_pairs={{0,1},{1,0},{2,3},{3,2},{4,5},{5,4},{6,7},{7,6},{8,9},{9,8},{10,11... | collective-permute-start | bytes 1572872 | tf_op jit(solution)/shard_map/ppermute | solution.py:186
  155.5 17.1 %collective-permute-start.19 = (bf16[64,1024]{1,0:T(8,128)(2,1)S(1)}, bf16[64,1024]{1,0:T(8,128)(2,1)S(1)}, u32[]{:S(2)}, u32[]{:S(2)}) collective-permute-start(bf16[64,1024]{1,0:T(8,128)(2,1)S(1)} %get-tuple-element.55), channel_id=1, source_target_pairs={{0,4},{1,5},{2,6},{3,7},{4,0},{5,1},{6,2},{7,3},{8,12},{9,13},{10,... | collective-permute-start | bytes 393224 | tf_op jit(solution)/shard_map/ppermute | solution.py:189
  156.0 16.7 %collective-permute-start.22 = (bf16[64,1024]{1,0:T(8,128)(2,1)S(1)}, bf16[64,1024]{1,0:T(8,128)(2,1)S(1)}, u32[]{:S(2)}, u32[]{:S(2)}) collective-permute-start(bf16[64,1024]{1,0:T(8,128)(2,1)S(1)} %get-tuple-element.56), channel_id=1, source_target_pairs={{0,2},{1,3},{2,4},{3,5},{4,6},{5,7},{6,0},{7,1},{8,10},{9,11},{10,... | collective-permute-start | bytes 393224 | tf_op jit(solution)/shard_map/ppermute | solution.py:189
  158.0 14.6 %collective-permute-start.24 = (bf16[64,1024]{1,0:T(8,128)(2,1)S(1)}, bf16[64,1024]{1,0:T(8,128)(2,1)S(1)}, u32[]{:S(2)}, u32[]{:S(2)}) collective-permute-start(bf16[64,1024]{1,0:T(8,128)(2,1)S(1)} %get-tuple-element.57), channel_id=1, source_target_pairs={{0,6},{1,7},{2,0},{3,1},{4,2},{5,3},{6,4},{7,5},{8,14},{9,15},{10,... | collective-permute-start | bytes 393224 | tf_op jit(solution)/shard_map/ppermute | solution.py:189
  159.9 16.9 %collective-permute-start.23 = (bf16[64,1024]{1,0:T(8,128)(2,1)S(1)}, bf16[64,1024]{1,0:T(8,128)(2,1)S(1)}, u32[]{:S(2)}, u32[]{:S(2)}) collective-permute-start(bf16[64,1024]{1,0:T(8,128)(2,1)S(1)} %get-tuple-element.58), channel_id=1, source_target_pairs={{0,4},{1,5},{2,6},{3,7},{4,0},{5,1},{6,2},{7,3},{8,12},{9,13},{10,... | collective-permute-start | bytes 393224 | tf_op jit(solution)/shard_map/ppermute | solution.py:189
  (34 other events, 268.9 us)
